TPU v7x, 32 devices: a whole 2x2x4 slice. The times are simulated.
32 devices in a mesh: rep: 2 (over y), gx: 4 (over x, core), gy: 4 (over z).
Axes of the slice: x: 2, y: 2, z: 4, core: 2. Of those that a mesh axis runs over, the one named last changes fastest.
Arguments:
- deltas: bfloat16 [2, 2, 3584, 14336], P('rep', None, 'gx', 'gy'), may hold values from -32 to 32
- params: float32 [2, 4, 4, 2, 4, 4, 112, 896], P(None, None, 'gx', 'rep', None, 'gy'), may hold values from -0.75 to 0.75
- momentum: float32 [2, 4, 4, 2, 4, 4, 112, 896], P(None, None, 'gx', 'rep', None, 'gy'), may hold values from -1.5 to 1.5
Outputs:
- new_params: float32 [2, 4, 4, 2, 4, 4, 112, 896], P(None, None, 'gx', 'rep', None, 'gy')
- new_momentum: float32 [2, 4, 4, 2, 4, 4, 112, 896], P(None, None, 'gx', 'rep', None, 'gy')
All inputs are finite; a program needn't handle non-finite values.
Results may differ from a plain program's by a relative error of at most 0.0003.
Values may be sent and summed in bfloat16 or wider, within the bound.
A program may use at most 128 MiB of HBM per device.

v0:
```python
import jax
import jax.numpy as jnp
from jax import lax
from jax.sharding import PartitionSpec as P

clip_level = 0.25
moment_decay = 0.9
outer_rate = 0.7
epsilon = 1e-06


def per_device(deltas, params, momentum):
    rows_split = lax.axis_size("gx")
    cols_split = lax.axis_size("gy")
    replicas = lax.axis_size("rep")
    matrices = deltas.shape[1]
    local_rows = deltas.shape[2]
    local_cols = deltas.shape[3]
    row_tile = local_rows // (rows_split * replicas)
    col_tile = local_cols // cols_split
    entries = matrices * local_rows * local_cols * rows_split * cols_split
    blocks = deltas.reshape(matrices, rows_split, replicas, row_tile, cols_split, col_tile)
    received = lax.all_to_all(blocks[None], "rep", split_axis=3, concat_axis=0, tiled=True)
    summed = jnp.sum(received, axis=0, dtype=jnp.float32)
    partial_value = summed / replicas
    squares = lax.psum(jnp.sum(partial_value * partial_value), ("rep", "gx", "gy"))
    mean_delta = lax.all_to_all(
        lax.all_to_all(partial_value, "gx", split_axis=1, concat_axis=1, tiled=True),
        "gy",
        split_axis=4,
        concat_axis=4,
        tiled=True,
    )
    root_mean = jnp.sqrt(squares / entries + epsilon)
    clip_scale = jnp.minimum(1.0, clip_level / root_mean)
    arranged = jnp.transpose(mean_delta, (0, 1, 2, 4, 3, 5)).reshape(params.shape)
    gradient = clip_scale * arranged
    new_momentum = moment_decay * momentum + gradient
    new_params = params - outer_rate * (gradient + moment_decay * new_momentum)
    return (new_params, new_momentum)


def solution(mesh):
    return jax.shard_map(
        per_device,
        mesh=mesh,
        in_specs=(
            P("rep", None, "gx", "gy"),
            P(None, None, "gx", "rep", None, "gy", None, None),
            P(None, None, "gx", "rep", None, "gy", None, None),
        ),
        out_specs=(
            P(None, None, "gx", "rep", None, "gy", None, None),
            P(None, None, "gx", "rep", None, "gy", None, None),
        ),
        check_vma=False,
    )
```

profile of v0, /device:TPU:0, one launch (start us, length us, event | category | flops | bytes accessed | tf_op | source)
XLA Modules:
  0.0 728.3 jit_solution(14214572394206877874)
XLA Ops:
  0.6 21.9 %broadcast_in_dim_reshape.3 = bf16[1,2,4,2,112,4,896]{6,5,4,3,2,1,0:T(4,128)(2,1)} reshape(bf16[1,2,896,3584]{3,2,1,0:T(8,128)(2,1)} %param.3) | data formatting | bytes 25690112 | tf_op jit(solution)/shard_map/broadcast_in_dim;reshape | solution.py:23
  22.6 7.8 %copy.20 = bf16[1,2,4,2,112,4,896]{6,5,4,2,1,0,3:T(4,128)(2,1)S(1)} copy(bf16[1,2,4,2,112,4,896]{6,5,4,3,2,1,0:T(4,128)(2,1)} %broadcast_in_dim_reshape.3) | data formatting | bytes 25690112 | tf_op jit(solution)/shard_map/broadcast_in_dim;reshape | solution.py:23
  30.4 146.6 %all_to_all.19 = bf16[1,2,4,2,112,4,896]{6,5,4,2,1,0,3:T(4,128)(2,1)} all-to-all(bf16[1,2,4,2,112,4,896]{6,5,4,2,1,0,3:T(4,128)(2,1)S(1)} %copy.20), channel_id=1, replica_groups=mesh['rep'=2,'gx'=4,'gy'=4] {'rep'}, dimensions={3} | all-to-all | bytes 25690112 | tf_op jit(solution)/shard_map/all_to_all | solution.py:23
  177.0 15.0 %convert_reduce_fusion = f32[2,4,112,4,896]{4,2,3,1,0:T(8,128)} fusion(bf16[1,2,4,2,112,4,896]{6,5,4,2,1,0,3:T(4,128)(2,1)} %all_to_all.19), kind=kLoop, calls=%fused_computation | loop fusion | flops 9633792 | bytes 25690112 | tf_op jit(solution)/shard_map/reduce_sum | solution.py:24
  192.1 15.7 %multiply_reduce_fusion = (f32[]{:T(128)}, f32[2,4,1,112,4,896]{5,4,3,1,0,2:T(4,128)}) fusion(f32[2,4,112,4,896]{4,2,3,1,0:T(8,128)} %convert_reduce_fusion), kind=kLoop, calls=%fused_computation.7 | loop fusion | flops 9633791 | bytes 25690116 | tf_op jit(solution)/shard_map/reduce_sum | solution.py:26
  207.8 10.6 %copy.23 = f32[2,4,1,112,4,896]{5,3,4,0,2,1:T(8,128)} copy(f32[2,4,1,112,4,896]{5,4,3,1,0,2:T(4,128)} %get-tuple-element.11) | data formatting | bytes 25690112 | tf_op jit(solution)/shard_map/div | solution.py:25
  218.5 150.4 %all_to_all.20 = f32[2,4,1,112,4,896]{5,3,4,0,2,1:T(8,128)} all-to-all(f32[2,4,1,112,4,896]{5,3,4,0,2,1:T(8,128)} %copy.23), channel_id=1, replica_groups=mesh['rep'=2,'gx'=4,'gy'=4] {'gx'}, dimensions={1} | all-to-all | bytes 25690112 | tf_op jit(solution)/shard_map/all_to_all | solution.py:28
  368.9 10.6 %copy.24 = f32[2,4,1,112,4,896]{5,3,1,0,2,4:T(8,128)} copy(f32[2,4,1,112,4,896]{5,3,4,0,2,1:T(8,128)} %all_to_all.20) | data formatting | bytes 25690112 | tf_op jit(solution)/shard_map/all_to_all | solution.py:28
  379.5 6.4 all-to-all-start.2
  385.9 298.0 %psum.7 = f32[]{:T(128)} all-reduce(f32[]{:T(128)} %get-tuple-element.10), channel_id=1, replica_groups=mesh['rep'=2,'gx'=4,'gy'=4] {'rep','gx','gy'}, use_global_device_ids=true, to_apply=%region_2.0 | all-reduce | flops 1 | bytes 8 | tf_op jit(solution)/shard_map/psum | solution.py:26
  684.6 0.0 all-to-all-done.2
  684.6 22.3 %bitcast_add_fusion.1 = (f32[2,4,1,1,4,1,112,896]{7,6,1,0,4,5,3,2:T(8,128)}, f32[2,4,1,1,4,1,112,896]{7,6,1,0,4,5,3,2:T(8,128)}) fusion(f32[2,4,1,1,4,1,112,896]{7,6,5,4,3,2,1,0:T(8,128)} %param.5, f32[2,4,1,112,4,896]{5,3,1,0,2,4:T(8,128)} %all-to-all-done.2, f32[]{:T(128)S(6)} %min_shard_map.3, f32[2,4,1,1,4,1,112,896]{7,6,5,4,3,2,1,0:T(8,128)} %param.4), kind=kLoop, calls=%fused_computation.3 | loop fusion | flops 22478848 | bytes 64225284 | tf_op jit(solution)/shard_map/add | solution.py:38
  706.9 10.7 %copy.28 = f32[2,4,1,1,4,1,112,896]{7,6,5,4,3,2,1,0:T(8,128)} copy(f32[2,4,1,1,4,1,112,896]{7,6,1,0,4,5,3,2:T(8,128)} %get-tuple-element.8) | data formatting | bytes 25690112
  717.6 10.7 %copy.27 = f32[2,4,1,1,4,1,112,896]{7,6,5,4,3,2,1,0:T(8,128)} copy(f32[2,4,1,1,4,1,112,896]{7,6,1,0,4,5,3,2:T(8,128)} %get-tuple-element.9) | data formatting | bytes 25690112
Async XLA Ops:
  379.5 305.1 %all-to-all-start.2 = ((f32[2,4,1,112,4,896]{5,3,1,0,2,4:T(8,128)}), f32[2,4,1,112,4,896]{5,3,1,0,2,4:T(8,128)}, u32[]{:S(2)}, u32[]{:S(2)}) async-start(f32[2,4,1,112,4,896]{5,3,1,0,2,4:T(8,128)} %copy.24), calls=%async_computation.2 | async-start | bytes 25690112 | tf_op jit(solution)/shard_map/all_to_all | solution.py:27
where the time goes:
time: 730 us; the launch traced here: 728 us
  blocking collectives  595 us (82%)
  local copies, waits for them, and re-layouts  72.4 us (10%)
  other arithmetic  53.1 us (7%)
    psum x1, blocking collectives, per_device(): lax.psum(jnp.sum(partial_value * partial_value), ('rep', 'gx', 'gy'))  298 us
    all_to_all x1, blocking collectives, per_device(): lax.all_to_all(partial_value, 'gx', split_axis=1, concat_axis=1, tiled=True)  150 us
    all_to_all x1, blocking collectives, per_device(): lax.all_to_all(blocks[None], 'rep', split_axis=3, concat_axis=0, tiled=True)  147 us
    another operation x2, local copies, waits for them, and re-layouts, per_device(): blocks[None]  29.8 us
    add x1, other arithmetic, per_device(): new_momentum = moment_decay * momentum + gradient  22.3 us
    unnamed x2, local copies, waits for them, and re-layouts  21.4 us
    reduce_sum x1, other arithmetic, per_device(): jnp.sum(partial_value * partial_value)  15.7 us
    reduce_sum x1, other arithmetic, per_device(): summed = jnp.sum(received, axis=0, dtype=jnp.float32)  15 us
  transfers between devices with their start and end apart: 1, of which 0 were waited for; matrix products, arithmetic and copies ran while one was open for 0% of the time, Pallas kernels for 0%

commit v1 on v0

--- a/solution.py
+++ b/solution.py
@@ -7,6 +7,13 @@
 moment_decay = 0.9
 outer_rate = 0.7
 epsilon = 1e-06
+
+
+def swap_blocks(x, mesh_axis, split, join):
+    count = lax.axis_size(mesh_axis)
+    parts = jnp.stack(jnp.split(x, count, axis=split), axis=0)
+    parts = lax.all_to_all(parts, mesh_axis, split_axis=0, concat_axis=0)
+    return jnp.concatenate(parts, axis=join)
 
 
 def per_device(deltas, params, momentum):
@@ -25,11 +32,7 @@
     partial_value = summed / replicas
     squares = lax.psum(jnp.sum(partial_value * partial_value), ("rep", "gx", "gy"))
     mean_delta = lax.all_to_all(
-        lax.all_to_all(partial_value, "gx", split_axis=1, concat_axis=1, tiled=True),
-        "gy",
-        split_axis=4,
-        concat_axis=4,
-        tiled=True,
+        swap_blocks(partial_value, "gx", 1, 1), "gy", split_axis=4, concat_axis=4, tiled=True
     )
     root_mean = jnp.sqrt(squares / entries + epsilon)
     clip_scale = jnp.minimum(1.0, clip_level / root_mean)

time: 730 us -> 735 us (level)
    another operation x0 -> x2, local copies, waits for them, and re-layouts: none -> 12.9 us  [swap_blocks(): parts = jnp.stack(jnp.split(x, count, axis=split), axis=0)]
    div x1 -> x0, local copies, waits for them, and re-layouts: 10.6 us -> none  [per_device(): partial_value = summed / replicas]
    all_to_all x1 -> x0, local copies, waits for them, and re-layouts: 10.6 us -> none  [per_device(): lax.all_to_all(partial_value, 'gx', split_axis=1, concat_axis=1, tiled=True)]
    reshape x0 -> x1, local copies, waits for them, and re-layouts: none -> 10.6 us  [swap_blocks(): return jnp.concatenate(parts, axis=join)]
where the time goes in v1:
time: 735 us; the launch traced here: 734 us
  blocking collectives  595 us (81%)
  local copies, waits for them, and re-layouts  74.7 us (10%)
  other arithmetic  56.2 us (8%)
    psum x1, blocking collectives, per_device(): lax.psum(jnp.sum(partial_value * partial_value), ('rep', 'gx', 'gy'))  298 us
    all_to_all x1, blocking collectives, swap_blocks(): parts = lax.all_to_all(parts, mesh_axis, split_axis=0, concat_axis=0)  150 us
    all_to_all x1, blocking collectives, per_device(): lax.all_to_all(blocks[None], 'rep', split_axis=3, concat_axis=0, tiled=True)  147 us
    another operation x2, local copies, waits for them, and re-layouts, per_device(): blocks[None]  29.8 us
    add x1, other arithmetic, per_device(): new_momentum = moment_decay * momentum + gradient  22.3 us
    unnamed x2, local copies, waits for them, and re-layouts  21.4 us
    reduce_sum x1, other arithmetic, per_device(): summed = jnp.sum(received, axis=0, dtype=jnp.float32)  15 us
  transfers between devices with their start and end apart: 1, of which 0 were waited for; matrix products, arithmetic and copies ran while one was open for 0% of the time, Pallas kernels for 0%

profile of v1, /device:TPU:0, one launch (start us, length us, event | category | flops | bytes accessed | tf_op | source)
XLA Modules:
  0.0 733.7 jit_solution(11662160768231156437)
XLA Ops:
  0.6 21.9 %broadcast_in_dim_reshape.3 = bf16[1,2,4,2,112,4,896]{6,5,4,3,2,1,0:T(4,128)(2,1)} reshape(bf16[1,2,896,3584]{3,2,1,0:T(8,128)(2,1)} %param.3) | data formatting | bytes 25690112 | tf_op jit(solution)/shard_map/broadcast_in_dim;reshape | solution.py:30
  22.6 7.8 %copy.29 = bf16[1,2,4,2,112,4,896]{6,5,4,2,1,0,3:T(4,128)(2,1)S(1)} copy(bf16[1,2,4,2,112,4,896]{6,5,4,3,2,1,0:T(4,128)(2,1)} %broadcast_in_dim_reshape.3) | data formatting | bytes 25690112 | tf_op jit(solution)/shard_map/broadcast_in_dim;reshape | solution.py:30
  30.4 146.6 %all_to_all.19 = bf16[1,2,4,2,112,4,896]{6,5,4,2,1,0,3:T(4,128)(2,1)} all-to-all(bf16[1,2,4,2,112,4,896]{6,5,4,2,1,0,3:T(4,128)(2,1)S(1)} %copy.29), channel_id=1, replica_groups=mesh['rep'=2,'gx'=4,'gy'=4] {'rep'}, dimensions={3} | all-to-all | bytes 25690112 | tf_op jit(solution)/shard_map/all_to_all | solution.py:30
  177.0 15.0 %convert_reduce_fusion = f32[2,4,112,4,896]{4,2,3,1,0:T(8,128)} fusion(bf16[1,2,4,2,112,4,896]{6,5,4,2,1,0,3:T(4,128)(2,1)} %all_to_all.19), kind=kLoop, calls=%fused_computation | loop fusion | flops 9633792 | bytes 25690112 | tf_op jit(solution)/shard_map/reduce_sum | solution.py:31
  192.1 12.6 %multiply_reduce_fusion = (f32[]{:T(128)}, f32[2,4,1,112,4,896]{5,4,3,1,0,2:T(4,128)S(1)}) fusion(f32[2,4,112,4,896]{4,2,3,1,0:T(8,128)} %convert_reduce_fusion), kind=kLoop, calls=%fused_computation.8 | loop fusion | flops 9633791 | bytes 25690116 | tf_op jit(solution)/shard_map/reduce_sum | solution.py:33
  204.7 2.2 slice_bitcast_fusion.3
  206.9 6.3 pad_maximum_fusion
  213.2 10.6 %copy.35 = f32[4,2,1,1,112,4,896]{6,4,5,1,3,2,0:T(8,128)} copy(f32[4,2,1,1,112,4,896]{6,5,4,1,3,2,0:T(4,128)} %pad_maximum_fusion) | data formatting | bytes 25690112 | tf_op jit(solution)/shard_map/stack | solution.py:14
  223.9 150.4 %all_to_all.20 = f32[4,2,1,1,112,4,896]{6,4,5,1,3,2,0:T(8,128)} all-to-all(f32[4,2,1,1,112,4,896]{6,4,5,1,3,2,0:T(8,128)} %copy.35), channel_id=1, replica_groups=mesh['rep'=2,'gx'=4,'gy'=4] {'gx'}, dimensions={0} | all-to-all | bytes 25690112 | tf_op jit(solution)/shard_map/all_to_all | solution.py:15
  374.3 10.6 %copy.36 = f32[2,4,1,112,4,896]{5,3,1,0,2,4:T(8,128)} copy(f32[2,4,1,112,4,896]{5,3,4,0,1,2:T(8,128)} %bitcast.32) | data formatting | bytes 25690112 | tf_op jit(solution)/shard_map/reshape | solution.py:16
  384.9 6.4 all-to-all-start.2
  391.3 298.0 %psum.7 = f32[]{:T(128)} all-reduce(f32[]{:T(128)} %get-tuple-element.10), channel_id=1, replica_groups=mesh['rep'=2,'gx'=4,'gy'=4] {'rep','gx','gy'}, use_global_device_ids=true, to_apply=%region_2.0 | all-reduce | flops 1 | bytes 8 | tf_op jit(solution)/shard_map/psum | solution.py:33
  690.0 0.0 all-to-all-done.2
  690.0 22.3 %bitcast_add_fusion.1 = (f32[2,4,1,1,4,1,112,896]{7,6,1,0,4,5,3,2:T(8,128)}, f32[2,4,1,1,4,1,112,896]{7,6,1,0,4,5,3,2:T(8,128)}) fusion(f32[2,4,1,1,4,1,112,896]{7,6,5,4,3,2,1,0:T(8,128)} %param.5, f32[2,4,1,112,4,896]{5,3,1,0,2,4:T(8,128)} %all-to-all-done.2, f32[]{:T(128)S(6)} %min_shard_map.3, f32[2,4,1,1,4,1,112,896]{7,6,5,4,3,2,1,0:T(8,128)} %param.4), kind=kLoop, calls=%fused_computation.4 | loop fusion | flops 22478848 | bytes 64225284 | tf_op jit(solution)/shard_map/add | solution.py:41
  712.3 10.7 %copy.40 = f32[2,4,1,1,4,1,112,896]{7,6,5,4,3,2,1,0:T(8,128)} copy(f32[2,4,1,1,4,1,112,896]{7,6,1,0,4,5,3,2:T(8,128)} %get-tuple-element.8) | data formatting | bytes 25690112
  723.0 10.7 %copy.39 = f32[2,4,1,1,4,1,112,896]{7,6,5,4,3,2,1,0:T(8,128)} copy(f32[2,4,1,1,4,1,112,896]{7,6,1,0,4,5,3,2:T(8,128)} %get-tuple-element.9) | data formatting | bytes 25690112
Async XLA Ops:
  384.9 305.1 %all-to-all-start.2 = ((f32[2,4,1,112,4,896]{5,3,1,0,2,4:T(8,128)}), f32[2,4,1,112,4,896]{5,3,1,0,2,4:T(8,128)}, u32[]{:S(2)}, u32[]{:S(2)}) async-start(f32[2,4,1,112,4,896]{5,3,1,0,2,4:T(8,128)} %copy.36), calls=%async_computation.2 | async-start | bytes 25690112 | tf_op jit(solution)/shard_map/all_to_all | solution.py:34
